TPU v7x, 32 devices: a 4x2x2 block of a 4x4x8 slice. The times are simulated.
32 devices in a mesh: dp: 4 (over y, z), tp: 8 (over x, core).
Axes of the slice: x: 4, y: 2, z: 2, core: 2. Of those that a mesh axis runs over, the one named last changes fastest.
The devices are a block of a 4x4x8 slice.
Arguments:
- hidden: bfloat16 [4, 3072, 1536], P('dp', 'tp'), parts along dimension 0
- targets: int32 [4, 3072], P('dp', 'tp'), parts along dimension 0
- norm_gain: bfloat16 [1536], replicated
- head_w: bfloat16 [151936, 1536], P('tp')
- temperature: float32 [], replicated
Outputs:
- output 1: float32 [4, 3072], P('dp', 'tp'), parts along dimension 0
- output 2: float32 [4, 3072], P('dp', 'tp'), parts along dimension 0
There are 4 independent parts. A program takes and returns all parts, laid end to end along the dimension named above; an argument that names none is the same for every part.
All inputs are finite; a program needn't handle non-finite values.
Results may differ from a plain program's by a relative error of at most 0.001.
Values are sent between devices in bfloat16 or wider.
A program may use at most 768 MiB of HBM per device.

v0:
```python
import jax
import jax.numpy as jnp
from jax import lax
from jax.sharding import PartitionSpec as P

NORM_EPS = 1e-6


def solution(mesh):
    def device_body(h_loc, target_loc, norm_gain, w_loc, value_a11):
        tok_loc = h_loc.shape[1]
        vocab_loc = w_loc.shape[0]
        shard_idx = lax.axis_index('tp')
        h_wide = h_loc.astype(jnp.float32)
        inv_rms = lax.rsqrt(jnp.mean(h_wide * h_wide, axis=-1, keepdims=True) + NORM_EPS)
        normed = (norm_gain.astype(jnp.float32) * h_wide * inv_rms).astype(jnp.bfloat16)
        normed_all = lax.all_gather(normed, 'tp', axis=1, tiled=True)
        target_all = lax.all_gather(target_loc, 'tp', axis=1, tiled=True)
        logits = jnp.einsum('rsd,vd->rsv', normed_all, w_loc, preferred_element_type=jnp.float32) / value_a11
        local_max = jnp.max(logits, axis=-1)
        top_val = lax.pmax(local_max, 'tp')
        exp_shift = jnp.exp(logits - top_val[..., None])
        sum_exp = jnp.sum(exp_shift, axis=-1)
        weighted = jnp.sum(exp_shift * logits, axis=-1)
        vocab_ids = lax.broadcasted_iota(jnp.int32, (1, 1, vocab_loc), 2) + shard_idx * vocab_loc
        target_logit = jnp.sum(jnp.where(vocab_ids == target_all[..., None], logits, 0.0), axis=-1)
        stacked = jnp.stack([sum_exp, weighted, target_logit])
        own_sums = lax.psum_scatter(stacked, 'tp', scatter_dimension=2, tiled=True)
        own_max = lax.dynamic_slice_in_dim(top_val, shard_idx * tok_loc, tok_loc, axis=1)
        log_norm = own_max + jnp.log(own_sums[0])
        return own_sums[2] - log_norm, log_norm - own_sums[1] / own_sums[0]

    return jax.shard_map(
        device_body,
        mesh=mesh,
        in_specs=(P('dp', 'tp', None), P('dp', 'tp'), P(), P('tp', None), P()),
        out_specs=(P('dp', 'tp'), P('dp', 'tp')),
        check_vma=False,
    )
```

profile of v0, /device:TPU:81, one launch (start us, length us, event | category | flops | bytes accessed | tf_op | source)
XLA Modules:
  0.0 428.9 jit_solution(2003221016079302322)
XLA Ops:
  7.2 0.1 all-gather.2.cloned.1.call-start
  7.2 0.7 convert_element_type.9
  7.9 1.6 fusion.4
  9.5 2.6 fusion.3
  12.1 0.1 all-gather.2.cloned.1.call-update
  12.2 0.1 reduce-scatter.4.cloned.1.call-start
  12.9 14.7 %all_gather.7 = s32[1,3072]{1,0:T(1,128)} all-gather(s32[1,384]{1,0:T(1,128)} %param.6), channel_id=1, replica_groups=mesh['dp'=4,'tp'=8] {'tp'}, dimensions={1}, use_global_device_ids=true | all-gather | bytes 13824 | tf_op jit(solution)/shard_map/all_gather | solution.py:18
  27.6 0.6 iota_add_fusion
  28.3 39.5 %all-gather.2.cloned.1.call-done = bf16[1,3072,1536]{2,1,0:T(8,128)(2,1)} async-done(((bf16[1,384,1536]{2,1,0:T(8,128)(2,1)}), bf16[1,3072,1536]{2,1,0:T(8,128)(2,1)}) %all-gather.2.cloned.1.call-update) | async-done | bytes 9437200 | tf_op jit(solution)/shard_map/all_gather | solution.py:17
  67.7 0.0 copy-start
  67.7 0.0 copy-start.1
  67.8 195.6 %fusion.6 = (f32[3072]{0:T(1024)S(1)}, f32[3072,18992]{0,1:T(8,128)}) fusion(f32[]{:T(128)S(6)} %copy.12, bf16[18992,1536]{1,0:T(8,128)(2,1)} %param.8, bf16[1,3072,1536]{2,1,0:T(8,128)(2,1)} %all-gather.2.cloned.1.call-done), kind=kOutput, calls=%fused_computation.20 | convolution fusion | flops 179347685376 | bytes 301166592 | tf_op jit(solution)/shard_map/rsd,vd->rsv/dot_general | solution.py:19
  263.4 20.9 %pmax.7 = f32[1,3072]{1,0:T(1,128)S(1)} all-reduce(f32[1,3072]{1,0:T(1,128)S(1)} %bitcast.31), channel_id=1, replica_groups=mesh['dp'=4,'tp'=8] {'tp'}, use_global_device_ids=true, to_apply=%region_2.0 | all-reduce | flops 3072 | bytes 24576 | tf_op jit(solution)/shard_map/pmax | solution.py:21
  284.3 0.0 copy-done
  284.3 0.0 copy-done.1
  284.3 93.4 %fusion = (f32[3072]{0:T(1024)S(1)}, f32[3072]{0:T(1024)S(1)}, f32[3072]{0:T(1024)S(1)}) fusion(f32[3072,18992]{0,1:T(8,128)} %get-tuple-element.11, f32[3072]{0:T(1024)S(1)} %bitcast.26, s32[3072]{0:T(1024)S(1)} %bitcast.30, s32[18992]{0:T(1024)S(1)} %copy-done), kind=kLoop, calls=%fused_computation.3 | loop fusion | flops 408394752 | bytes 233511104 | tf_op jit(solution)/shard_map/reduce_sum | solution.py:23
  377.8 4.5 %copy.7 = f32[3,1,3072]{1,0,2:T(4,128)} copy(f32[3,1,3072]{2,1,0:T(1,128)S(1)} %pad_maximum_fusion) | data formatting | bytes 73728
  382.3 7.9 %bitcast_reduce_fusion = f32[3072,3]{1,0:T(8,128)} fusion(f32[3,1,3072]{1,0,2:T(4,128)} %copy.7), kind=kLoop, calls=%fused_computation.6 | loop fusion | bytes 73728
  390.2 0.1 reduce-scatter.4.cloned.1.call-update
  390.2 29.0 %reduce-scatter.4.cloned.1.call-done = f32[384,3]{1,0:T(8,128)} async-done(((f32[3072,3]{1,0:T(8,128)}), f32[384,3]{1,0:T(8,128)}) %reduce-scatter.4.cloned.1.call-update) | async-done | bytes 4624
  419.3 1.4 reshape_bitcast_fusion
  420.7 0.4 fusion.5
  421.1 0.1 copy.10
  421.2 0.1 copy.11
  421.3 0.1 copy.9
  421.4 0.6 bitcast_subtract_fusion
  (2 shorter events, 0.0 us)
Async XLA Ops:
  7.2 60.6 %all-gather.2.cloned.1.call-start = ((), (), s32[]{:S(2)}) async-start(), calls=%async_computation.1 | async-start | bytes 10616832 | tf_op jit(solution)/shard_map/all_gather | solution.py:17
  12.2 407.1 %reduce-scatter.4.cloned.1.call-start = ((), (), s32[]{:S(2)}) async-start(), calls=%async_computation.2 | async-start | bytes 1769472
  67.7 216.6 %copy-start = (s32[18992]{0:T(1024)S(1)}, s32[18992]{0:T(1024)}, u32[]{:S(2)}) copy-start(s32[18992]{0:T(1024)} %iota_add_fusion) | copy-start | bytes 227908
  67.7 216.6 %copy-start.1 = (s32[1,3072]{1,0:T(1,128)S(1)}, s32[1,3072]{1,0:T(1,128)}, u32[]{:S(2)}) copy-start(s32[1,3072]{1,0:T(1,128)} %all_gather.7) | copy-start | bytes 36868
Sparse Core Ops, SparseCore 0:
  12.3 55.4 all-gather.1
  390.4 28.8 reduce-scatter.3
where the time goes:
time: 431 us; the launch traced here: 429 us
  matrix products  196 us (45%)
  other arithmetic  99.6 us (23%)
  waiting for transfers between devices  68.6 us (16%)
  blocking collectives  35.6 us (8%)
  between operations  14.8 us (3%)
  local copies, waits for them, and re-layouts  14.5 us (3%)
    dot_general x1, matrix products, device_body(): jnp.einsum('rsd,vd->rsv', normed_all, w_loc, preferred_element_type=jnp.f...  196 us
    reduce_sum x1, other arithmetic, device_body(): sum_exp = jnp.sum(exp_shift, axis=-1)  93.4 us
    all_gather x1, waiting for transfers between devices, device_body(): normed_all = lax.all_gather(normed, 'tp', axis=1, tiled=True)  39.5 us
    unnamed x3, waiting for transfers between devices  29.1 us
    pmax x1, blocking collectives, device_body(): top_val = lax.pmax(local_max, 'tp')  20.9 us
    all_gather x1, blocking collectives, device_body(): target_all = lax.all_gather(target_loc, 'tp', axis=1, tiled=True)  14.7 us
    unnamed x10, local copies, waits for them, and re-layouts  14.1 us
  transfers between devices with their start and end apart: 2, of which 2 were waited for; matrix products, arithmetic and copies ran while one was open for 0% of the time, Pallas kernels for 0%

commit v1 on v0

v1 whole, which is shorter than its diff:
```python
import functools

import jax
import jax.numpy as jnp
from jax import lax
from jax.experimental import pallas as pl
from jax.experimental.pallas import tpu as pltpu
from jax.sharding import PartitionSpec as P

NORM_EPS = 1e-6
LOG2E = 1.4426950408889634
LOWEST = -3.4028234e38
SIDE = 256
M_ROWS = 432
PIECE = 48
SUBS = 2
RELAY_TRIP = 7
MESH = pl.DeviceIdType.MESH


def _kernel(dims, h_ref, tgt_ref, gain_ref, tau_ref, w_ref, lp_ref, ent_ref,
            h_buf, x_all, tgt_all, w_buf, z_buf, st_m, st_s, st_w, st_t, c_buf, stage, inbox,
            h_sem, w_sem, x_send, x_recv, t_send, t_recv, s_send, s_recv):
    n_tp, tok, depth, vocab = dims
    chips = n_tp // 2
    pair = 2 * tok
    blocks = pair // SIDE
    n_k = depth // SIDE
    sub_rows = 2 * M_ROWS
    tile_rows = SUBS * sub_rows
    n_tiles = -(-vocab // tile_rows)
    overlap = n_tiles * tile_rows - vocab
    units = SUBS * blocks
    n_stats = chips * blocks
    me = lax.axis_index('tp')
    x_pos, core = lax.div(me, 2), lax.rem(me, 2)

    def device(hops, other):
        return {'tp': lax.rem(x_pos + hops, chips) * 2 + (1 - core if other else core)}

    hops_of = {0: 0, 1: chips - 1, 2: 1, 3: 2}
    seen_as = {0: 0, 1: 2, 2: 1, 3: 3}
    peers = [(g, o) for g in range(chips) for o in (0, 1) if (g, o) != (0, 0)]

    def row_start(j):
        return pl.multiple_of(jnp.minimum(j * tile_rows, vocab - tile_rows), 16)

    def w_copy(q, s):
        j = lax.rem(q, n_tiles)
        return pltpu.make_async_copy(
            w_ref.at[pl.ds(pl.multiple_of(row_start(j) + s * sub_rows, 16), sub_rows)],
            w_buf.at[lax.rem(q, 2), pl.ds(s * sub_rows, sub_rows)],
            w_sem.at[lax.rem(q, 2), s],
        )

    h_copy = pltpu.make_async_copy(h_ref, h_buf, h_sem)
    h_copy.start()
    for s in range(SUBS):
        w_copy(0, s).start()
    barrier = pltpu.get_barrier_semaphore()
    for g, o in peers:
        pl.semaphore_signal(barrier, inc=1, device_id=device(hops_of[g], o), device_id_type=MESH)

    c_buf[...] = LOG2E / jnp.full(c_buf.shape, tau_ref[0, 0], jnp.float32)
    st_m[...] = jnp.full(st_m.shape, LOWEST, jnp.float32)
    for st in (st_s, st_w, st_t):
        st[...] = jnp.zeros(st.shape, jnp.float32)

    own_rows = pl.ds(pl.multiple_of(core * tok, 16), tok)
    own_lanes = pl.ds(pl.multiple_of(core * tok, 128), tok)
    h_copy.wait()

    norm_rows = 64

    @pl.loop(0, tok // norm_rows)
    def _(r):
        h = h_buf[pl.ds(pl.multiple_of(r * norm_rows, 16), norm_rows), :].astype(jnp.float32)
        inv = lax.rsqrt(jnp.mean(h * h, axis=-1, keepdims=True) + NORM_EPS)
        x = (gain_ref[...].astype(jnp.float32) * h * inv).astype(jnp.bfloat16)
        x_all[0, pl.ds(pl.multiple_of(core * tok + r * norm_rows, 16), norm_rows), :] = x

    pl.semaphore_wait(barrier, len(peers))

    def x_copy(src_g, dst_g, hops, other, send):
        return pltpu.make_async_remote_copy(
            src_ref=x_all.at[src_g, own_rows],
            dst_ref=x_all.at[dst_g, own_rows],
            send_sem=x_send.at[send],
            recv_sem=x_recv.at[dst_g * 2 + other],
            device_id=device(hops, other),
            device_id_type=MESH,
        )

    def x_arrival(g, other):
        rows = pl.ds(pl.multiple_of((1 - core if other else core) * tok, 16), tok)
        return pltpu.make_async_remote_copy(
            src_ref=x_all.at[g, rows],
            dst_ref=x_all.at[g, rows],
            send_sem=x_send.at[0],
            recv_sem=x_recv.at[g * 2 + other],
            device_id=device(0, 1),
            device_id_type=MESH,
        )

    def t_copy(g, o):
        n = g * 2 + o
        return pltpu.make_async_remote_copy(
            src_ref=tgt_ref,
            dst_ref=tgt_all.at[seen_as[g], :, own_lanes],
            send_sem=t_send.at[n],
            recv_sem=t_recv.at[seen_as[g] * 2 + o],
            device_id=device(hops_of[g], o),
            device_id_type=MESH,
        )

    own_copies = [x_copy(0, 1, 1, 0, 1), x_copy(0, 2, chips - 1, 0, 2), x_copy(0, 0, 0, 1, 0)]
    for copy in own_copies:
        copy.start()
    for g, o in peers:
        t_copy(g, o).start()
    tgt_all[0, :, own_lanes] = tgt_ref[...]

    far = x_copy(jnp.where(core == 0, 1, 2), 3, jnp.where(core == 0, 1, chips - 1), 0, 3)
    relays = [x_copy(1, 1, 0, 1, 4), x_copy(2, 2, 0, 1, 5), x_copy(3, 3, 0, 1, 6)]

    def t_wait(g, o):
        n = seen_as[g] * 2 + o
        pltpu.make_async_remote_copy(
            src_ref=tgt_ref,
            dst_ref=tgt_all.at[g, :, pl.ds(pl.multiple_of((1 - core if o else core) * tok, 128), tok)],
            send_sem=t_send.at[n],
            recv_sem=t_recv.at[g * 2 + o],
            device_id=device(0, 1),
            device_id_type=MESH,
        ).wait_recv()

    for g, o in peers:
        t_wait(g, o)
    x_arrival(0, 1).wait_recv()

    sublane = lax.broadcasted_iota(jnp.int32, (8, SIDE), 0)

    def place(t):
        first = t < n_tiles
        u = jnp.maximum(t - n_tiles, 0)
        j = jnp.where(first, t, lax.div(u, chips - 1))
        g = jnp.where(first, 0, 1 + lax.rem(u, chips - 1))
        q = jnp.where(first, t, n_tiles + lax.div(u, chips - 1))
        fresh = jnp.logical_or(first, lax.rem(u, chips - 1) == 0)
        return j, g, q, fresh

    def drain(accs, stat, base, bias, target):
        m_old = st_m[stat]
        top = m_old
        z = z_buf[accs]
        if bias is not None:
            head = z[:overlap].reshape(overlap // 8, 8, SIDE) + bias
            top = jnp.maximum(top, jnp.max(head, axis=0))
            z = z[overlap:]
        top = jnp.maximum(top, jnp.max(z.reshape(-1, 8, SIDE), axis=0))
        c = c_buf[...]
        alpha = jnp.exp2((m_old - top) * c)
        st_m[stat] = top
        state = [st_s[stat] * alpha, st_w[stat] * alpha, st_t[stat]]
        where = target - sublane - base
        for r in range(0, sub_rows, PIECE):
            z = z_buf[accs, pl.ds(r, PIECE), :].reshape(PIECE // 8, 8, SIDE)
            zb = z
            if bias is not None and r == 0:
                zb = jnp.concatenate([z[:overlap // 8] + bias, z[overlap // 8:]], axis=0)
            p = jnp.exp2((zb - top) * c)
            state[0] = state[0] + jnp.sum(p, axis=0)
            state[1] = state[1] + jnp.sum(p * z, axis=0)
            for i in range(PIECE // 8):
                state[2] = jnp.where(where == r + 8 * i, z[i], state[2])
        st_s[stat], st_w[stat], st_t[stat] = state

    def body():
        z_buf[1] = jnp.zeros(z_buf.shape[1:], jnp.float32)

        def trip(t, carry):
            j, g, q, fresh = place(t)
            slot = lax.rem(q, 2)

            @pl.when(fresh)
            def _():
                @pl.when(q + 1 < 2 * n_tiles)
                def _():
                    for s in range(SUBS):
                        w_copy(q + 1, s).start()
                for s in range(SUBS):
                    w_copy(q, s).wait()

            @pl.when(t == RELAY_TRIP)
            def _():
                x_arrival(1, 0).wait_recv()
                x_arrival(2, 0).wait_recv()
                far.start()
                relays[0].start()
                relays[1].start()

            @pl.when(t == n_tiles)
            def _():
                x_arrival(1, 1).wait_recv()
                x_arrival(2, 1).wait_recv()

            @pl.when(t == n_tiles + 1)
            def _():
                x_arrival(3, 0).wait_recv()
                relays[2].start()

            @pl.when(t == n_tiles + 2)
            def _():
                x_arrival(3, 1).wait_recv()

            shard_base = me * vocab + row_start(j)
            bias = jnp.where(j == n_tiles - 1, LOWEST, 0.0).astype(jnp.float32)
            pj, pg, _, _ = place(jnp.maximum(t - 1, 0))
            for i in range(units):
                s, b = divmod(i, blocks)
                z_buf[i % 2] = lax.dot_general(
                    w_buf[slot, pl.ds(s * sub_rows, sub_rows), :], x_all[g, pl.ds(b * SIDE, SIDE), :],
                    (((1,), (1,)), ((), ())), preferred_element_type=jnp.float32)
                if i == 0:
                    stat = jnp.where(t == 0, n_stats, pg * blocks + blocks - 1)
                    base = me * vocab + row_start(pj) + (SUBS - 1) * sub_rows
                    target = tgt_all[pg, :, (blocks - 1) * SIDE:blocks * SIDE]
                    drain(1, stat, base, None, target)
                else:
                    ps, pb = divmod(i - 1, blocks)
                    target = tgt_all[g, :, pb * SIDE:(pb + 1) * SIDE]
                    drain((i - 1) % 2, g * blocks + pb, shard_base + ps * sub_rows,
                          bias if ps == 0 else None, target)
            return carry

        trips = n_tiles * chips
        lax.fori_loop(0, trips, trip, 0)
        pj, pg, _, _ = place(trips - 1)
        drain(1, pg * blocks + blocks - 1, me * vocab + row_start(pj) + (SUBS - 1) * sub_rows, None,
              tgt_all[pg, :, (blocks - 1) * SIDE:blocks * SIDE])

    body()

    c1 = c_buf[0:1, :]
    for g in range(chips):
        for b in range(blocks):
            n, lanes = g * blocks + b, slice(b * SIDE, (b + 1) * SIDE)
            m = st_m[n]
            top = jnp.max(m, axis=0, keepdims=True)
            f = jnp.exp2((m - top) * c1)
            stage[g, 0:1, lanes] = top
            stage[g, 1:2, lanes] = jnp.sum(st_s[n] * f, axis=0, keepdims=True)
            stage[g, 2:3, lanes] = jnp.sum(st_w[n] * f, axis=0, keepdims=True)
            stage[g, 3:4, lanes] = jnp.sum(st_t[n], axis=0, keepdims=True)
            stage[g, 4:8, lanes] = jnp.zeros((4, SIDE), jnp.float32)

    def s_copy(g, o):
        n = g * 2 + o
        lanes = pl.ds(pl.multiple_of((1 - core if o else core) * tok, 128), tok)
        return pltpu.make_async_remote_copy(
            src_ref=stage.at[g, :, lanes],
            dst_ref=inbox.at[seen_as[g] * 2 + o],
            send_sem=s_send.at[n],
            recv_sem=s_recv.at[seen_as[g] * 2 + o],
            device_id=device(hops_of[g], o),
            device_id_type=MESH,
        )

    s_copies = [s_copy(g, o) for g, o in peers]
    for copy in s_copies:
        copy.start()
    inbox[0] = stage[0, :, own_lanes]
    for copy in s_copies:
        copy.wait()
    got = [inbox[n] for n in range(n_tp)]
    top = functools.reduce(jnp.maximum, [x[0:1] for x in got])
    c2 = jnp.concatenate([c1, c1], axis=1)[:, :tok]
    scales = [jnp.exp2((x[0:1] - top) * c2) for x in got]
    total = functools.reduce(jnp.add, [x[1:2] * f for x, f in zip(got, scales)])
    weighted = functools.reduce(jnp.add, [x[2:3] * f for x, f in zip(got, scales)])
    target = functools.reduce(jnp.add, [x[3:4] for x in got])
    tau = jnp.full(top.shape, tau_ref[0, 0], jnp.float32)
    log_norm = top / tau + jnp.log(total)
    lp_ref[...] = target / tau - log_norm
    ent_ref[...] = log_norm - (weighted / total) / tau

    for copy in own_copies + [far] + relays:
        copy.wait_send()
    for g, o in peers:
        t_copy(g, o).wait_send()


def solution(mesh):
    n_tp = mesh.shape['tp']

    def device_body(h_loc, target_loc, norm_gain, w_loc, tau):
        _, tok, depth = h_loc.shape
        vocab = w_loc.shape[0]
        pair, chips = 2 * tok, n_tp // 2
        blocks = pair // SIDE
        n_stats = chips * blocks
        any_space = pl.BlockSpec(memory_space=pl.ANY)
        vmem = pl.BlockSpec(memory_space=pltpu.VMEM)
        stat = pltpu.VMEM((n_stats + 1, 8, SIDE), jnp.float32)
        dma = pltpu.SemaphoreType.DMA
        return pl.pallas_call(
            functools.partial(_kernel, (n_tp, tok, depth, vocab)),
            out_shape=(jax.ShapeDtypeStruct((1, tok), jnp.float32),) * 2,
            in_specs=[any_space, vmem, vmem, pl.BlockSpec(memory_space=pltpu.SMEM), any_space],
            out_specs=(vmem, vmem),
            scratch_shapes=[
                pltpu.VMEM((tok, depth), jnp.bfloat16),
                pltpu.VMEM((chips, pair, depth), jnp.bfloat16),
                pltpu.VMEM((chips, 1, pair), jnp.int32),
                pltpu.VMEM((2, SUBS * 2 * M_ROWS, depth), jnp.bfloat16),
                pltpu.VMEM((2, 2 * M_ROWS, SIDE), jnp.float32),
                stat, stat, stat, stat,
                pltpu.VMEM((8, SIDE), jnp.float32),
                pltpu.VMEM((chips, 8, pair), jnp.float32),
                pltpu.VMEM((n_tp, 8, tok), jnp.float32),
                dma(()), dma((2, SUBS)), dma((7,)), dma((n_tp,)), dma((n_tp,)), dma((n_tp,)), dma((n_tp,)), dma((n_tp,)),
            ],
            compiler_params=pltpu.CompilerParams(
                collective_id=0, has_side_effects=True, vmem_limit_bytes=60 * 1024 * 1024),
        )(h_loc[0], target_loc, norm_gain.reshape(1, depth), tau.reshape(1, 1), w_loc)

    return jax.shard_map(
        device_body,
        mesh=mesh,
        in_specs=(P('dp', 'tp', None), P('dp', 'tp'), P(), P('tp', None), P()),
        out_specs=(P('dp', 'tp'), P('dp', 'tp')),
        check_vma=False,
    )
```

time: 431 us -> 246 us (0.57)
  Pallas kernels: 0 us -> 241 us
  matrix products: 196 us -> 0 us
  other arithmetic: 99.6 us -> 0 us
  waiting for transfers between devices: 68.6 us -> 0 us
  blocking collectives: 35.6 us -> 0 us
  between operations: 14.8 us -> 1.29 us
  local copies, waits for them, and re-layouts: 14.5 us -> 3.72 us
    pallas_call x0 -> x1, Pallas kernels: none -> 241 us  [device_body(): pl.pallas_call(functools.partial(_kernel, (n_tp, tok, depth, vocab)), out...]
    dot_general x1 -> x0, matrix products: 196 us -> none  [device_body(): jnp.einsum('rsd,vd->rsv', normed_all, w_loc, preferred_element_type=jnp.f...]
    reduce_sum x2 -> x0, other arithmetic: 95 us -> none  [the longest x1 93.4 us: device_body(): sum_exp = jnp.sum(exp_shift, axis=-1)]
    all_gather x1 -> x0, waiting for transfers between devices: 39.5 us -> none  [device_body(): normed_all = lax.all_gather(normed, 'tp', axis=1, tiled=True)]
    unnamed x3 -> x0, waiting for transfers between devices: 29.1 us -> none
    pmax x1 -> x0, blocking collectives: 20.9 us -> none  [device_body(): top_val = lax.pmax(local_max, 'tp')]
    all_gather x1 -> x0, blocking collectives: 14.7 us -> none  [device_body(): target_all = lax.all_gather(target_loc, 'tp', axis=1, tiled=True)]
    unnamed x10 -> x2, local copies, waits for them, and re-layouts: 14.1 us -> 2.45 us
  transfers between devices with their start and end apart: 2 -> 0, of which waited for: 2 -> 0; matrix products, arithmetic and copies ran while one was open for 0% -> 0% of each run, Pallas kernels for 0% -> 0%
where the time goes in v1:
time: 246 us
  Pallas kernels  241 us (98%)
  local copies, waits for them, and re-layouts  3.72 us (2%)
    pallas_call x1, Pallas kernels, device_body(): pl.pallas_call(functools.partial(_kernel, (n_tp, tok, depth, vocab)), out...  241 us

profile of v1, /device:TPU:81, one launch (start us, length us, event | category | flops | bytes accessed | tf_op | source)
XLA Modules:
  0.0 245.6 jit_solution(970897816032094248)
XLA Ops:
  1.3 1.3 reshape.10.gain_ref
  2.6 240.6 %shard_map.68 = (f32[1,384]{1,0:T(1,128)}, f32[1,384]{1,0:T(1,128)}) custom-call(bf16[384,1536]{1,0:T(8,128)(2,1)} %bitcast.3, s32[1,384]{1,0:T(1,128)} %tgt_ref.1, bf16[1,1536]{1,0:T(2,128)(2,1)} %reshape.10.gain_ref, f32[1,1]{1,0:T(1,128)} %bitcast.2.tau_ref, bf16[18992,1536]{1,0:T(8,128)(2,1)} %w_ref.1), custom_call_target="tpu_custom_call" | custom-call | tf_op jit(solution)/shard_map/pallas_call | solution.py:306
  243.1 1.2 copy.10
  244.4 1.2 copy.11

commit v2 on v0

v2 whole, which is shorter than its diff:
```python
import functools

import jax
import jax.numpy as jnp
from jax import lax
from jax.experimental import pallas as pl
from jax.experimental.pallas import tpu as pltpu
from jax.sharding import PartitionSpec as P

NORM_EPS = 1e-6
LOG2E = 1.4426950408889634
LOWEST = -3.4028234e38
SIDE = 256
UNIT_ROWS = 864
SUBS = 2
PIECE = 48
NORM_ROWS = 64
W_SLOTS = 4
MESH = pl.DeviceIdType.MESH

OWNER = {(0, 1): (0, 1), (1, 0): (-1, 0), (1, 1): (1, 0), (2, 0): (-1, 1), (2, 1): (1, 1), (3, 0): (2, 0), (3, 1): (2, 1)}
SEEN_AS = {(0, 1): (0, 1), (1, 0): (1, 1), (1, 1): (1, 0), (2, 0): (2, 1), (2, 1): (2, 0), (3, 0): (3, 0), (3, 1): (3, 1)}


def _kernel(dims, h_ref, tgt_ref, gain_ref, tau_ref, w_ref, out_ref,
            h_buf, x_all, tgt_all, w_buf, z_buf, z_top, st_m, st_s, st_w, st_t, c_buf, stage, inbox,
            h_sem, w_sem, x_send, x_recv, t_send, t_recv, s_send, s_recv):
    n_tp, tok, depth, vocab = dims
    chips = n_tp // 2
    pair = 2 * tok
    blocks = pair // SIDE
    tile_rows = SUBS * UNIT_ROWS
    n_tiles = -(-vocab // tile_rows)
    overlap = n_tiles * tile_rows - vocab
    half_units = SUBS * blocks
    n_stats = chips * blocks
    me = lax.axis_index('tp')
    x_pos, core = lax.div(me, 2), lax.rem(me, 2)

    def device(hops, other):
        return {'tp': lax.rem(x_pos + hops + chips, chips) * 2 + (1 - core if other else core)}

    def row_start(j):
        return pl.multiple_of(jnp.minimum(j * tile_rows, vocab - tile_rows), 16)

    def w_copy(q, s):
        slot = lax.rem(q, W_SLOTS)
        return pltpu.make_async_copy(
            w_ref.at[pl.ds(pl.multiple_of(row_start(lax.rem(q, n_tiles)) + s * UNIT_ROWS, 16), UNIT_ROWS)],
            w_buf.at[slot, pl.ds(s * UNIT_ROWS, UNIT_ROWS)],
            w_sem.at[slot, s],
        )

    def w_start(q):
        for s in range(SUBS):
            w_copy(q, s).start()

    def w_wait(q):
        for s in range(SUBS):
            w_copy(q, s).wait()

    h_copy = pltpu.make_async_copy(h_ref, h_buf, h_sem)
    h_copy.start()
    w_start(0)
    w_start(1)
    barrier = pltpu.get_barrier_semaphore()
    for hops, other in OWNER.values():
        pl.semaphore_signal(barrier, inc=1, device_id=device(hops, other), device_id_type=MESH)

    c_buf[...] = LOG2E / jnp.full(c_buf.shape, tau_ref[0, 0], jnp.float32)
    st_m[...] = jnp.full(st_m.shape, LOWEST, jnp.float32)
    for st in (st_s, st_w, st_t):
        st[...] = jnp.zeros(st.shape, jnp.float32)
    z_top[...] = jnp.zeros(z_top.shape, jnp.float32)
    for n in (2, 3):
        z_buf[n] = jnp.zeros(z_buf.shape[1:], jnp.float32)

    h_copy.wait()
    gain = gain_ref[...].astype(jnp.float32).reshape(1, depth)

    @pl.loop(0, tok // NORM_ROWS)
    def _(r):
        rows = pl.ds(pl.multiple_of(r * NORM_ROWS, 16), NORM_ROWS)
        h = h_buf[rows, :].astype(jnp.float32)
        inv = lax.rsqrt(jnp.mean(h * h, axis=-1, keepdims=True) + NORM_EPS)
        x_all[0, rows, :] = (gain * h * inv).astype(jnp.bfloat16)

    pl.semaphore_wait(barrier, len(OWNER))

    def chunk(p, f):
        return x_all.at[p, pl.ds(f * tok if isinstance(f, int) else pl.multiple_of(f * tok, 16), tok)]

    def x_copy(src, dst, hops, other, send):
        return pltpu.make_async_remote_copy(
            src_ref=chunk(*src),
            dst_ref=chunk(*dst),
            send_sem=x_send.at[send],
            recv_sem=x_recv.at[dst[0] * 2 + dst[1]],
            device_id=device(hops, other),
            device_id_type=MESH,
        )

    def x_wait(p, f):
        x_copy((p, f), (p, f), 0, 1, 0).wait_recv()

    def t_copy(where):
        p, f = SEEN_AS[where]
        return pltpu.make_async_remote_copy(
            src_ref=tgt_ref,
            dst_ref=tgt_all.at[p, :, pl.ds(f * tok, tok)],
            send_sem=t_send.at[where[0] * 2 + where[1]],
            recv_sem=t_recv.at[p * 2 + f],
            device_id=device(*OWNER[where]),
            device_id_type=MESH,
        )

    t_copies = {where: t_copy(where) for where in OWNER}
    t_waits = {SEEN_AS[where]: copy for where, copy in t_copies.items()}
    for copy in t_copies.values():
        copy.start()
    own_copies = [x_copy((0, 0), (0, 1), 0, 1, 0), x_copy((0, 0), (1, 0), 1, 0, 1), x_copy((0, 0), (1, 1), -1, 0, 2)]
    for copy in own_copies:
        copy.start()
    tgt_all[0, :, 0:tok] = tgt_ref[...]

    far = x_copy((1, jnp.where(core == 0, 0, 1)), (3, 0), jnp.where(core == 0, 1, -1), 0, 3)
    to_other = [x_copy((1, 0), (2, 0), 0, 1, 4), x_copy((1, 1), (2, 1), 0, 1, 5), x_copy((3, 0), (3, 1), 0, 1, 6)]

    t_waits[(0, 1)].wait_recv()
    x_wait(0, 1)

    sublane = lax.broadcasted_iota(jnp.int32, (8, SIDE), 0)

    def place(h):
        late = h >= 3 * n_tiles
        first = h < n_tiles
        u = jnp.maximum(h - n_tiles, 0)
        j = jnp.where(first, h, jnp.where(late, h - 3 * n_tiles, lax.div(u, 2)))
        g = jnp.where(first, 0, jnp.where(late, 3, 1 + lax.rem(u, 2)))
        q = jnp.where(first, h, jnp.where(late, h - n_tiles, n_tiles + lax.div(u, 2)))
        return j, g, q

    def drain(slot, stat, base, bias, target):
        m_old = st_m[stat]
        top = jnp.maximum(m_old, z_top[slot])
        if bias is not None:
            head = z_buf[slot, 0:overlap, :].reshape(overlap // 8, 8, SIDE) + bias
            top = jnp.maximum(top, jnp.max(head, axis=0))
        c = c_buf[...]
        alpha = jnp.exp2((m_old - top) * c)
        st_m[stat] = top
        total, weighted, hit = st_s[stat] * alpha, st_w[stat] * alpha, st_t[stat]
        row = target - sublane - base
        for r in range(0, UNIT_ROWS, PIECE):
            z = z_buf[slot, pl.ds(r, PIECE), :].reshape(PIECE // 8, 8, SIDE)
            zb = z
            if bias is not None and r == 0:
                zb = jnp.concatenate([z[:overlap // 8] + bias, z[overlap // 8:]], axis=0)
            p = jnp.exp2((zb - top) * c)
            total = total + jnp.sum(p, axis=0)
            weighted = weighted + jnp.sum(p * z, axis=0)
            for i in range(PIECE // 8):
                hit = jnp.where(row == r + 8 * i, z[i], hit)
        st_s[stat], st_w[stat], st_t[stat] = total, weighted, hit

    def high(t):
        return place(2 * t + 1)[2]

    trips = n_tiles * chips // 2

    def drain_last(t, i, valid):
        j, g, _ = place(2 * t + 1)
        s, b = divmod(i, blocks)
        stat = g * blocks + b if valid is None else jnp.where(valid, g * blocks + b, n_stats)
        drain(2 + (i - (half_units - 2)), stat, me * vocab + row_start(j) + s * UNIT_ROWS, None,
              tgt_all[g, :, b * SIDE:(b + 1) * SIDE])

    def trip(t, carry):
        now, before, after = high(t), high(t - 1), high(t + 1)
        before = jnp.where(t == 0, -1, before)
        after = jnp.where(t == trips - 1, now, after)
        for n in (1, 2):
            @pl.when(now + n <= after)
            def _():
                w_start(now + n)
        for n in (1, 0):
            @pl.when(now - n > before)
            def _():
                w_wait(now - n)

        @pl.when(t == (n_tiles - 1) // 2)
        def _():
            for f in (0, 1):
                t_waits[(1, f)].wait_recv()
                x_wait(1, f)
            for copy in (far, to_other[0], to_other[1]):
                copy.start()

        @pl.when(t == (n_tiles - 1) // 2 + 1)
        def _():
            for f in (0, 1):
                t_waits[(2, f)].wait_recv()
                x_wait(2, f)

        @pl.when(t == n_tiles)
        def _():
            x_wait(3, 0)
            to_other[2].start()

        @pl.when(t == 3 * n_tiles // 2)
        def _():
            for f in (0, 1):
                t_waits[(3, f)].wait_recv()
            x_wait(3, 1)

        halves = [place(2 * t), place(2 * t + 1)]
        bias = [jnp.where(j == n_tiles - 1, LOWEST, 0.0).astype(jnp.float32) for j, _, _ in halves]
        for i in range(0, 2 * half_units, 2):
            for n in (i, i + 1):
                e, (s, b) = n // half_units, divmod(n % half_units, blocks)
                _, g, q = halves[e]
                z = lax.dot_general(
                    w_buf[lax.rem(q, W_SLOTS), pl.ds(s * UNIT_ROWS, UNIT_ROWS), :],
                    x_all[g, pl.ds(b * SIDE, SIDE), :],
                    (((1,), (1,)), ((), ())), preferred_element_type=jnp.float32)
                z_buf[n % 4] = z
                z_top[n % 4] = jnp.max(z[overlap if s == 0 else 0:].reshape(-1, 8, SIDE), axis=0)
            for n in (i - 2, i - 1):
                if n < 0:
                    drain_last(jnp.maximum(t - 1, 0), half_units + n, t > 0)
                else:
                    e, (s, b) = n // half_units, divmod(n % half_units, blocks)
                    j, g, _ = halves[e]
                    drain(n % 4, g * blocks + b, me * vocab + row_start(j) + s * UNIT_ROWS,
                          bias[e] if s == 0 else None, tgt_all[g, :, b * SIDE:(b + 1) * SIDE])
        return carry

    lax.fori_loop(0, trips, trip, 0)
    for n in (half_units - 2, half_units - 1):
        drain_last(trips - 1, n, None)

    c1 = c_buf[0:1, :]
    for g in range(chips):
        for b in range(blocks):
            n, lanes = g * blocks + b, slice(b * SIDE, (b + 1) * SIDE)
            m = st_m[n]
            top = jnp.max(m, axis=0, keepdims=True)
            f = jnp.exp2((m - top) * c1)
            stage[g, 0:1, lanes] = top
            stage[g, 1:2, lanes] = jnp.sum(st_s[n] * f, axis=0, keepdims=True)
            stage[g, 2:3, lanes] = jnp.sum(st_w[n] * f, axis=0, keepdims=True)
            stage[g, 3:4, lanes] = jnp.sum(st_t[n], axis=0, keepdims=True)
            stage[g, 4:8, lanes] = jnp.zeros((4, SIDE), jnp.float32)

    def s_copy(where):
        (p, f), (dp, df) = where, SEEN_AS[where]
        return pltpu.make_async_remote_copy(
            src_ref=stage.at[p, :, pl.ds(f * tok, tok)],
            dst_ref=inbox.at[dp * 2 + df],
            send_sem=s_send.at[p * 2 + f],
            recv_sem=s_recv.at[dp * 2 + df],
            device_id=device(*OWNER[where]),
            device_id_type=MESH,
        )

    s_copies = [s_copy(where) for where in OWNER]
    for copy in s_copies:
        copy.start()
    inbox[0] = stage[0, :, 0:tok]
    for copy in s_copies:
        copy.wait()
    got = [inbox[n] for n in range(n_tp)]
    top = functools.reduce(jnp.maximum, [x[0:1] for x in got])
    c2 = jnp.concatenate([c1, c1], axis=1)[:, :tok]
    scales = [jnp.exp2((x[0:1] - top) * c2) for x in got]
    out_ref[0:1, :] = top
    out_ref[1:2, :] = functools.reduce(jnp.add, [x[1:2] * f for x, f in zip(got, scales)])
    out_ref[2:3, :] = functools.reduce(jnp.add, [x[2:3] * f for x, f in zip(got, scales)])
    out_ref[3:4, :] = functools.reduce(jnp.add, [x[3:4] for x in got])

    for copy in own_copies + [far] + to_other + list(t_copies.values()):
        copy.wait_send()


def solution(mesh):
    n_tp = mesh.shape['tp']

    def device_body(h_loc, target_loc, norm_gain, w_loc, tau):
        _, tok, depth = h_loc.shape
        vocab = w_loc.shape[0]
        pair, chips = 2 * tok, n_tp // 2
        blocks = pair // SIDE
        any_space = pl.BlockSpec(memory_space=pl.ANY)
        vmem = pl.BlockSpec(memory_space=pltpu.VMEM)
        stat = pltpu.VMEM((chips * blocks + 1, 8, SIDE), jnp.float32)
        dma = pltpu.SemaphoreType.DMA
        out = pl.pallas_call(
            functools.partial(_kernel, (n_tp, tok, depth, vocab)),
            out_shape=jax.ShapeDtypeStruct((4, tok), jnp.float32),
            in_specs=[any_space, vmem, vmem, pl.BlockSpec(memory_space=pltpu.SMEM), any_space],
            out_specs=vmem,
            scratch_shapes=[
                pltpu.VMEM((tok, depth), jnp.bfloat16),
                pltpu.VMEM((chips, pair, depth), jnp.bfloat16),
                pltpu.VMEM((chips, 1, pair), jnp.int32),
                pltpu.VMEM((W_SLOTS, SUBS * UNIT_ROWS, depth), jnp.bfloat16),
                pltpu.VMEM((4, UNIT_ROWS, SIDE), jnp.float32),
                pltpu.VMEM((4, 8, SIDE), jnp.float32),
                stat, stat, stat, stat,
                pltpu.VMEM((8, SIDE), jnp.float32),
                pltpu.VMEM((chips, 8, pair), jnp.float32),
                pltpu.VMEM((n_tp, 8, tok), jnp.float32),
                dma(()), dma((W_SLOTS, SUBS)), dma((7,)), dma((n_tp,)), dma((n_tp,)), dma((n_tp,)), dma((n_tp,)),
                dma((n_tp,)),
            ],
            compiler_params=pltpu.CompilerParams(
                collective_id=0, has_side_effects=True, vmem_limit_bytes=60 * 1024 * 1024),
        )(h_loc[0], target_loc, norm_gain, tau.reshape(1, 1), w_loc)
        top, total, weighted, target = (out[n:n + 1] for n in range(4))
        log_norm = top / tau + jnp.log(total)
        return target / tau - log_norm, log_norm - (weighted / total) / tau

    return jax.shard_map(
        device_body,
        mesh=mesh,
        in_specs=(P('dp', 'tp', None), P('dp', 'tp'), P(), P('tp', None), P()),
        out_specs=(P('dp', 'tp'), P('dp', 'tp')),
        check_vma=False,
    )
```

time: 431 us -> 220 us (0.51)
  Pallas kernels: 0 us -> 216 us
  matrix products: 196 us -> 0 us
  other arithmetic: 99.6 us -> 2.64 us
  waiting for transfers between devices: 68.6 us -> 0 us
  blocking collectives: 35.6 us -> 0 us
  local copies, waits for them, and re-layouts: 14.5 us -> 0 us
  between operations: 14.8 us -> 1.29 us
    pallas_call x0 -> x1, Pallas kernels: none -> 216 us  [device_body(): pl.pallas_call(functools.partial(_kernel, (n_tp, tok, depth, vocab)), out...]
    dot_general x1 -> x0, matrix products: 196 us -> none  [device_body(): jnp.einsum('rsd,vd->rsv', normed_all, w_loc, preferred_element_type=jnp.f...]
    reduce_sum x2 -> x0, other arithmetic: 95 us -> none  [the longest x1 93.4 us: device_body(): sum_exp = jnp.sum(exp_shift, axis=-1)]
    all_gather x1 -> x0, waiting for transfers between devices: 39.5 us -> none  [device_body(): normed_all = lax.all_gather(normed, 'tp', axis=1, tiled=True)]
    unnamed x3 -> x0, waiting for transfers between devices: 29.1 us -> none
    pmax x1 -> x0, blocking collectives: 20.9 us -> none  [device_body(): top_val = lax.pmax(local_max, 'tp')]
    all_gather x1 -> x0, blocking collectives: 14.7 us -> none  [device_body(): target_all = lax.all_gather(target_loc, 'tp', axis=1, tiled=True)]
    unnamed x10 -> x0, local copies, waits for them, and re-layouts: 14.1 us -> none
  transfers between devices with their start and end apart: 2 -> 0, of which waited for: 2 -> 0; matrix products, arithmetic and copies ran while one was open for 0% -> 0% of each run, Pallas kernels for 0% -> 0%
where the time goes in v2:
time: 220 us
  Pallas kernels  216 us (98%)
  other arithmetic  2.64 us (1%)
    pallas_call x1, Pallas kernels, device_body(): pl.pallas_call(functools.partial(_kernel, (n_tp, tok, depth, vocab)), out...  216 us

profile of v2, /device:TPU:81, one launch (start us, length us, event | category | flops | bytes accessed | tf_op | source)
XLA Modules:
  0.0 219.8 jit_solution(11798657150459914262)
XLA Ops:
  1.3 215.9 %shard_map.68 = f32[4,384]{1,0:T(4,128)} custom-call(bf16[384,1536]{1,0:T(8,128)(2,1)} %bitcast.3, s32[1,384]{1,0:T(1,128)} %tgt_ref.1, bf16[1536]{0:T(1024)(128)(2,1)} %gain_ref.1, f32[1,1]{1,0:T(1,128)} %bitcast.2.tau_ref, bf16[18992,1536]{1,0:T(8,128)(2,1)} %w_ref.1), custom_call_target="tpu_custom_call" | custom-call | tf_op jit(solution)/shard_map/pallas_call | solution.py:297
  217.2 1.4 divide_subtract_fusion.1
  218.6 1.3 divide_subtract_fusion
